TPU v7x, 256 devices: a whole 4x4x8 slice. The times are simulated.
256 devices in a mesh: dp: 128 (over y, x_hi, z, core), mp: 2 (over x_lo).
Axes of the slice: x: 4 (x_hi: 2, x_lo: 2; x = x_hi * 2 + x_lo), y: 4, z: 8, core: 2. Of those that a mesh axis runs over, the one named last changes fastest.
Arguments:
- dino_tokens: bfloat16 [65536, 1024], P('dp', 'mp'), may hold values from -6 to 6
- siglip_tokens: bfloat16 [65536, 1152], P('dp', 'mp'), may hold values from -6 to 6
- dino_norm_one: float32 [1024], replicated, may hold values from 0.25 to 1.75
- dino_qkv: bfloat16 [1024, 3, 1024], P('dp', None, 'mp'), may hold values from -6.05625 to 6.05625
- dino_out: bfloat16 [1024, 1024], P('mp', 'dp'), may hold values from -0.1875 to 0.1875
- dino_norm_two: float32 [1024], replicated, may hold values from 0.25 to 1.75
- dino_up: bfloat16 [1024, 4096], P('dp', 'mp'), may hold values from -0.1875 to 0.1875
- dino_down: bfloat16 [4096, 1024], P('mp', 'dp'), may hold values from -0.09375 to 0.09375
- siglip_norm_one: float32 [1152], replicated, may hold values from 0.25 to 1.75
- siglip_qkv: bfloat16 [1152, 3, 1152], P('dp', None, 'mp'), may hold values from -5.709887 to 5.709887
- siglip_out: bfloat16 [1152, 1152], P('mp', 'dp'), may hold values from -0.1875 to 0.1875
- siglip_norm_two: float32 [1152], replicated, may hold values from 0.25 to 1.75
- siglip_up: bfloat16 [1152, 4304], P('dp', 'mp'), may hold values from -0.1875 to 0.1875
- siglip_down: bfloat16 [4304, 1152], P('mp', 'dp'), may hold values from -0.09375 to 0.09375
Outputs:
- dino_result: bfloat16 [65536, 1024], P('dp', 'mp')
- siglip_result: bfloat16 [65536, 1152], P('dp', 'mp')
All inputs are finite; a program needn't handle non-finite values.
Results may differ from a plain program's by a relative error of at most 0.012.
Values may be sent and summed in bfloat16 or wider, within the bound.
A program may use at most 128 MiB of HBM per device.

v0:
```python
import math
import jax
import jax.numpy as jnp
from jax import lax
from jax.sharding import PartitionSpec as P

HEADS = 16
PATCHES = 256
EPS = 1e-06


def from_everyone(shard, axis):
    size = lax.axis_size(axis)
    return lax.all_to_all(
        jnp.broadcast_to(shard[None], (size, *shard.shape)), axis, 0, 0, tiled=True
    )


def laid_out(pieces, dim):
    shape = list(pieces.shape[1:])
    shape[dim] *= pieces.shape[0]
    return jnp.moveaxis(pieces, 0, dim).reshape(shape)


def gathered_copies(shard, axis, dim):
    pieces = from_everyone(shard, axis)
    return laid_out(pieces, dim)


def split_up(shard, dim, size):
    shape = shard.shape
    pieces = shard.reshape(*shape[:dim], size, shape[dim] // size, *shape[dim + 1 :])
    return jnp.moveaxis(pieces, dim, 0)


def sum_at_owner(shard, axis, dim):
    pieces = split_up(shard, dim, lax.axis_size(axis))
    arrived = lax.all_to_all(pieces, axis, split_axis=0, concat_axis=0, tiled=True)
    return arrived.astype(jnp.float32).sum(axis=0)


def layer_norm(values, gain):
    values = values.astype(jnp.float32)
    center = values - jnp.mean(values, axis=-1, keepdims=True)
    spread = jnp.mean(center * center, axis=-1, keepdims=True)
    return (center * lax.rsqrt(spread + EPS) * gain).astype(jnp.bfloat16)


def encoder(tokens, norm_one, qkv_weight, out_weight, norm_two, up_weight, down_weight, approx):
    rows, local_width = tokens.shape
    whole = gathered_copies(tokens, "mp", 1)
    width = whole.shape[1]
    head_size = width // HEADS
    local_heads = qkv_weight.shape[2] // head_size
    scale = 1.0 / math.sqrt(head_size)
    normed = layer_norm(whole, norm_one)

    def fold_rows(source, piece):
        count = piece.shape[0]
        return jnp.dot(source, piece.reshape(count, -1), preferred_element_type=jnp.float32)

    qkv = fold_rows(normed, lax.all_gather(qkv_weight, "dp", axis=0, tiled=True))
    qkv = qkv.astype(jnp.bfloat16).reshape(rows // PATCHES, PATCHES, 3, local_heads, head_size)
    query = qkv[:, :, 0]
    keys = qkv[:, :, 1]
    values = qkv[:, :, 2]
    scores = jnp.einsum("fqhd,fkhd->fhqk", query, keys, preferred_element_type=jnp.float32) * scale
    top = jnp.max(scores, axis=-1, keepdims=True)
    expo = jnp.exp(scores - top)
    probs = (expo / jnp.sum(expo, axis=-1, keepdims=True)).astype(jnp.bfloat16)
    context = jnp.einsum("fhqk,fkhd->fqhd", probs, values, preferred_element_type=jnp.float32)
    context = context.astype(jnp.bfloat16).reshape(rows, local_heads * head_size)
    partial_attn = jnp.dot(
        context,
        lax.all_gather(out_weight, "dp", axis=1, tiled=True),
        preferred_element_type=jnp.float32,
    )
    share = sum_at_owner(partial_attn.astype(jnp.bfloat16), "mp", 1)
    middle = (tokens.astype(jnp.float32) + share).astype(jnp.bfloat16)
    middle_whole = gathered_copies(middle, "mp", 1)
    second = layer_norm(middle_whole, norm_two)
    raised = fold_rows(second, lax.all_gather(up_weight, "dp", axis=0, tiled=True))
    hidden = jax.nn.gelu(raised, approximate=approx).astype(jnp.bfloat16)
    partial_mlp = jnp.dot(
        hidden,
        lax.all_gather(down_weight, "dp", axis=1, tiled=True),
        preferred_element_type=jnp.float32,
    )
    mlp_part = sum_at_owner(partial_mlp.astype(jnp.bfloat16), "mp", 1)
    return (middle.astype(jnp.float32) + mlp_part).astype(jnp.bfloat16)


def local(
    dino_tokens,
    siglip_tokens,
    dino_norm_one,
    dino_qkv,
    dino_out,
    dino_norm_two,
    dino_up,
    dino_down,
    siglip_norm_one,
    siglip_qkv,
    siglip_out,
    siglip_norm_two,
    siglip_up,
    siglip_down,
):
    dino_result = encoder(
        dino_tokens, dino_norm_one, dino_qkv, dino_out, dino_norm_two, dino_up, dino_down, False
    )
    siglip_result = encoder(
        siglip_tokens,
        siglip_norm_one,
        siglip_qkv,
        siglip_out,
        siglip_norm_two,
        siglip_up,
        siglip_down,
        True,
    )
    return (dino_result, siglip_result)


def solution(mesh):
    in_specs = (
        P("dp", "mp"),
        P("dp", "mp"),
        P(),
        P("dp", None, "mp"),
        P("mp", "dp"),
        P(),
        P("dp", "mp"),
        P("mp", "dp"),
        P(),
        P("dp", None, "mp"),
        P("mp", "dp"),
        P(),
        P("dp", "mp"),
        P("mp", "dp"),
    )
    out_specs = (P("dp", "mp"), P("dp", "mp"))
    return jax.shard_map(local, mesh=mesh, in_specs=in_specs, out_specs=out_specs, check_vma=False)
```

profile of v0, /device:TPU:1, one launch (start us, length us, event | category | flops | bytes accessed | tf_op | source)
XLA Modules:
  0.0 1024.6 jit_solution(13799758242859776503)
XLA Ops:
  14.2 3.6 all-to-all-start
  17.8 11.6 %all-to-all-done = bf16[2,512,512]{1,2,0:T(8,128)(2,1)S(1)} async-done(((bf16[2,512,512]{1,2,0:T(8,128)(2,1)}), bf16[2,512,512]{1,2,0:T(8,128)(2,1)S(1)}, u32[]{:S(2)}, u32[]{:S(2)}) %all-to-all-start) | async-done | bytes 1048608 | tf_op jit(solution)/shard_map/all_to_all | solution.py:14
  30.6 3.6 all-to-all-start.4
  36.1 90.8 %all-gather.12.cloned.1.call-done = bf16[1024,3,512]{2,0,1:T(8,128)(2,1)} async-done(((bf16[8,3,512]{2,0,1:T(8,128)(2,1)}), bf16[1024,3,512]{2,0,1:T(8,128)(2,1)}) %all-gather.12.cloned.1.call-update) | async-done | bytes 3145744 | tf_op jit(solution)/shard_map/all_gather | solution.py:62
  126.8 4.7 copy.44
  131.5 4.1 convolution_convert_fusion.2
  148.3 3.2 fusion.103
  152.7 78.1 %all-gather.14.cloned.1.call-done = bf16[512,1024]{0,1:T(8,128)(2,1)} async-done(((bf16[512,8]{0,1:T(8,128)(2,1)}), bf16[512,1024]{0,1:T(8,128)(2,1)}) %all-gather.14.cloned.1.call-update) | async-done | bytes 1048592 | tf_op jit(solution)/shard_map/all_gather | solution.py:75
  233.9 3.6 all-to-all-start.1
  238.5 12.6 %all-to-all-done.1 = bf16[2,512,512]{2,1,0:T(8,128)(2,1)S(1)} async-done(((bf16[2,512,512]{2,1,0:T(8,128)(2,1)}), bf16[2,512,512]{2,1,0:T(8,128)(2,1)S(1)}, u32[]{:S(2)}, u32[]{:S(2)}) %all-to-all-start.1) | async-done | bytes 1048608 | tf_op jit(solution)/shard_map/all_to_all | solution.py:38
  252.8 4.0 all-to-all-start.2
  258.6 91.0 %all-gather.22.cloned.1.call-done = bf16[128,9,576]{2,1,0:T(8,128)(2,1)} async-done(((bf16[1,9,576]{2,1,0:T(8,128)(2,1)}), bf16[128,9,576]{2,1,0:T(8,128)(2,1)}) %all-gather.22.cloned.1.call-update) | async-done | bytes 1327120 | tf_op jit(solution)/shard_map/all_gather | solution.py:75
  349.6 4.1 reshape.167
  353.9 118.7 %all-gather.20.cloned.1.call-done = bf16[1152,3,576]{2,1,0:T(4,128)(2,1)} async-done(((bf16[9,3,576]{2,1,0:T(4,128)(2,1)}), bf16[1152,3,576]{2,1,0:T(4,128)(2,1)}) %all-gather.20.cloned.1.call-update) | async-done | bytes 3981328 | tf_op jit(solution)/shard_map/all_gather | solution.py:62
  472.6 11.3 %copy.54 = bf16[1152,3,576]{0,2,1:T(8,128)(2,1)} copy(bf16[1152,3,576]{2,1,0:T(4,128)(2,1)} %all-gather.20.cloned.1.call-done) | data formatting | bytes 7962624 | tf_op jit(solution)/shard_map/all_gather | solution.py:62
  484.0 5.8 convolution_convert_fusion
  489.8 4.8 reshape.160
  498.0 3.2 fusion.104
  505.3 3.7 all-to-all-start.5
  510.7 13.2 %all-to-all-done.5 = bf16[2,512,576]{1,2,0:T(8,128)(2,1)S(1)} async-done(((bf16[2,512,576]{1,2,0:T(8,128)(2,1)}), bf16[2,512,576]{1,2,0:T(8,128)(2,1)S(1)}, u32[]{:S(2)}, u32[]{:S(2)}) %all-to-all-start.5) | async-done | bytes 1179680 | tf_op jit(solution)/shard_map/all_to_all | solution.py:38
  525.5 3.8 all-to-all-start.6
  529.3 63.4 %all-gather.16.cloned.1.call-done = bf16[1024,2048]{1,0:T(8,128)(2,1)} async-done(((bf16[8,2048]{1,0:T(8,128)(2,1)}), bf16[1024,2048]{1,0:T(8,128)(2,1)}) %all-gather.16.cloned.1.call-update) | async-done | bytes 4194320 | tf_op jit(solution)/shard_map/all_gather | solution.py:82
  592.7 120.0 %all-gather.18.cloned.1.call-done = bf16[2048,1024]{0,1:T(8,128)(2,1)} async-done(((bf16[2048,8]{0,1:T(8,128)(2,1)}), bf16[2048,1024]{0,1:T(8,128)(2,1)}) %all-gather.18.cloned.1.call-update) | async-done | bytes 4194320 | tf_op jit(solution)/shard_map/all_gather | solution.py:86
  712.7 17.9 %fusion.53 = bf16[512,1024]{1,0:T(8,128)(2,1)} fusion(bf16[2048,1024]{0,1:T(8,128)(2,1)} %all-gather.18.cloned.1.call-done, bf16[512,1024]{0,1:T(8,128)(2,1)} %fusion.46, bf16[1024,2048]{1,0:T(8,128)(2,1)} %all-gather.16.cloned.1.call-done), kind=kOutput, calls=%fused_computation.79 | convolution fusion | flops 4363649024 | bytes 10485760 | tf_op jit(solution)/shard_map/dot_general | solution.py:84
  733.0 4.5 all-to-all-start.3
  739.5 103.9 %all-gather.24.cloned.1.call-done = bf16[128,9,2152]{2,1,0:T(8,128)(2,1)} async-done(((bf16[1,9,2152]{2,1,0:T(8,128)(2,1)}), bf16[128,9,2152]{2,1,0:T(8,128)(2,1)}) %all-gather.24.cloned.1.call-update) | async-done | bytes 4958224 | tf_op jit(solution)/shard_map/all_gather | solution.py:82
  843.4 9.1 reshape.169
  852.5 121.5 %all-gather.26.cloned.1.call-done = bf16[128,9,2152]{2,1,0:T(8,128)(2,1)} async-done(((bf16[1,9,2152]{2,1,0:T(8,128)(2,1)}), bf16[128,9,2152]{2,1,0:T(8,128)(2,1)}) %all-gather.26.cloned.1.call-update) | async-done | bytes 4958224 | tf_op jit(solution)/shard_map/all_gather | solution.py:86
  974.1 9.1 reshape.171
  983.2 12.2 %convolution_convert_fusion.3 = bf16[512,1152]{1,0:T(8,128)(2,1)} fusion(bf16[1152,2152]{1,0:T(8,128)(2,1)} %reshape.171, bf16[512,1152]{0,1:T(8,128)(2,1)S(1)} %copy-done.5, bf16[1152,2152]{1,0:T(8,128)(2,1)} %reshape.169), kind=kOutput, calls=%fused_computation.41 | convolution fusion | flops 5087711232 | bytes 12275712 | tf_op jit(solution)/shard_map/dot_general | solution.py:84
  997.8 3.6 all-to-all-start.7
  1003.9 12.4 %all-to-all-done.7 = bf16[2,512,576]{1,2,0:T(8,128)(2,1)S(1)} async-done(((bf16[2,512,576]{1,2,0:T(8,128)(2,1)}), bf16[2,512,576]{1,2,0:T(8,128)(2,1)S(1)}, u32[]{:S(2)}, u32[]{:S(2)}) %all-to-all-start.7) | async-done | bytes 1179680 | tf_op jit(solution)/shard_map/all_to_all | solution.py:38
  (96 shorter events, 52.7 us)
Async XLA Ops:
  7.2 10.7 %copy-start.9 = (f32[1024]{0:T(1024)S(1)}, f32[1024]{0:T(1024)}, u32[]{:S(2)}) copy-start(f32[1024]{0:T(1024)} %param.16) | copy-start | bytes 12292
  7.2 22.3 %copy-start = (bf16[512,576]{0,1:T(8,128)(2,1)S(1)}, bf16[512,576]{0,1:T(8,128)(2,1)}, u32[]{:S(2)}) copy-start(bf16[512,576]{0,1:T(8,128)(2,1)} %param.15) | copy-start | bytes 1769476
  7.2 119.6 %all-gather.12.cloned.1.call-start = ((), (), s32[]{:S(2)}) async-start(), calls=%async_computation.8 | async-start | bytes 3170304 | tf_op jit(solution)/shard_map/all_gather | solution.py:62
  7.9 222.9 %all-gather.14.cloned.1.call-start = ((), (), s32[]{:S(2)}) async-start(), calls=%async_computation.9 | async-start | bytes 1056768 | tf_op jit(solution)/shard_map/all_gather | solution.py:75
  8.7 340.9 %all-gather.22.cloned.1.call-start = ((), (), s32[]{:S(2)}) async-start(), calls=%async_computation.13 | async-start | bytes 2641920 | tf_op jit(solution)/shard_map/all_gather | solution.py:75
  9.4 463.2 %all-gather.20.cloned.1.call-start = ((), (), s32[]{:S(2)}) async-start(), calls=%async_computation.12 | async-start | bytes 5944320 | tf_op jit(solution)/shard_map/all_gather | solution.py:62
  10.0 582.7 %all-gather.16.cloned.1.call-start = ((), (), s32[]{:S(2)}) async-start(), calls=%async_computation.10 | async-start | bytes 4227072 | tf_op jit(solution)/shard_map/all_gather | solution.py:82
  10.6 702.2 %all-gather.18.cloned.1.call-start = ((), (), s32[]{:S(2)}) async-start(), calls=%async_computation.11 | async-start | bytes 4227072 | tf_op jit(solution)/shard_map/all_gather | solution.py:86
  11.1 832.3 %all-gather.24.cloned.1.call-start = ((), (), s32[]{:S(2)}) async-start(), calls=%async_computation.14 | async-start | bytes 8982528 | tf_op jit(solution)/shard_map/all_gather | solution.py:82
  14.2 15.2 %all-to-all-start = ((bf16[2,512,512]{1,2,0:T(8,128)(2,1)}), bf16[2,512,512]{1,2,0:T(8,128)(2,1)S(1)}, u32[]{:S(2)}, u32[]{:S(2)}) async-start(bf16[2,512,512]{1,2,0:T(8,128)(2,1)} %broadcast_in_dim.8), calls=%async_computation | async-start | bytes 2097152 | tf_op jit(solution)/shard_map/all_to_all | solution.py:14
  30.6 203.3 %all-to-all-start.4 = ((bf16[2,512,576]{1,2,0:T(8,128)(2,1)}), bf16[2,512,576]{1,2,0:T(8,128)(2,1)S(1)}, u32[]{:S(2)}, u32[]{:S(2)}) async-start(bf16[2,512,576]{1,2,0:T(8,128)(2,1)} %broadcast_in_dim.10), calls=%async_computation.4 | async-start | bytes 2359296 | tf_op jit(solution)/shard_map/all_to_all | solution.py:14
  152.6 85.7 %copy-start.7 = (f32[1152]{0:T(1024)S(1)}, f32[1152]{0:T(1024)}, u32[]{:S(2)}) copy-start(f32[1152]{0:T(1024)} %param.22) | copy-start | bytes 13828
  232.8 18.5 %copy-start.2 = (bf16[512,512]{1,0:T(8,128)(2,1)S(1)}, bf16[512,512]{1,0:T(8,128)(2,1)}, u32[]{:S(2)}) copy-start(bf16[512,512]{1,0:T(8,128)(2,1)} %param.14) | copy-start | bytes 1572868
  233.9 17.2 %all-to-all-start.1 = ((bf16[2,512,512]{2,1,0:T(8,128)(2,1)}), bf16[2,512,512]{2,1,0:T(8,128)(2,1)S(1)}, u32[]{:S(2)}, u32[]{:S(2)}) async-start(bf16[2,512,512]{2,1,0:T(8,128)(2,1)} %bitcast.102), calls=%async_computation.1 | async-start | bytes 2097152 | tf_op jit(solution)/shard_map/all_to_all | solution.py:38
  237.5 736.6 %all-gather.26.cloned.1.call-start = ((), (), s32[]{:S(2)}) async-start(), calls=%async_computation.15 | async-start | bytes 8982528 | tf_op jit(solution)/shard_map/all_gather | solution.py:86
  252.8 100.9 %all-to-all-start.2 = ((bf16[2,512,512]{1,2,0:T(8,128)(2,1)}), bf16[2,512,512]{1,2,0:T(8,128)(2,1)S(1)}, u32[]{:S(2)}, u32[]{:S(2)}) async-start(bf16[2,512,512]{1,2,0:T(8,128)(2,1)} %broadcast_in_dim.9), calls=%async_computation.2 | async-start | bytes 2097152 | tf_op jit(solution)/shard_map/all_to_all | solution.py:14
  353.9 130.0 %copy-start.4 = (bf16[2,512,576]{1,2,0:T(8,128)(2,1)S(1)}, bf16[2,512,576]{1,2,0:T(8,128)(2,1)}, u32[]{:S(2)}) copy-start(bf16[2,512,576]{1,2,0:T(8,128)(2,1)} %fusion.32) | copy-start | bytes 3538948
  501.2 1.4 copy-start.3
  502.6 6.8 copy-start.8
  505.3 18.8 %copy-start.1 = (bf16[512,576]{0,1:T(8,128)(2,1)S(1)}, bf16[512,576]{0,1:T(8,128)(2,1)}, u32[]{:S(2)}) copy-start(bf16[512,576]{0,1:T(8,128)(2,1)} %param.15) | copy-start | bytes 1769476
  505.3 18.6 %all-to-all-start.5 = ((bf16[2,512,576]{1,2,0:T(8,128)(2,1)}), bf16[2,512,576]{1,2,0:T(8,128)(2,1)S(1)}, u32[]{:S(2)}, u32[]{:S(2)}) async-start(bf16[2,512,576]{1,2,0:T(8,128)(2,1)} %bitcast.21), calls=%async_computation.5 | async-start | bytes 2359296 | tf_op jit(solution)/shard_map/all_to_all | solution.py:38
  525.5 207.5 %all-to-all-start.6 = ((bf16[2,512,576]{1,2,0:T(8,128)(2,1)}), bf16[2,512,576]{1,2,0:T(8,128)(2,1)S(1)}, u32[]{:S(2)}, u32[]{:S(2)}) async-start(bf16[2,512,576]{1,2,0:T(8,128)(2,1)} %broadcast_in_dim.11), calls=%async_computation.6 | async-start | bytes 2359296 | tf_op jit(solution)/shard_map/all_to_all | solution.py:14
  730.7 7.4 copy-start.6
  733.0 264.8 %all-to-all-start.3 = ((bf16[2,512,512]{2,1,0:T(8,128)(2,1)}), bf16[2,512,512]{2,1,0:T(8,128)(2,1)}, u32[]{:S(2)}, u32[]{:S(2)}) async-start(bf16[2,512,512]{2,1,0:T(8,128)(2,1)} %bitcast.103), calls=%async_computation.3 | async-start | bytes 2097152 | tf_op jit(solution)/shard_map/all_to_all | solution.py:38
  852.5 130.7 %copy-start.5 = (bf16[512,1152]{0,1:T(8,128)(2,1)S(1)}, bf16[512,1152]{0,1:T(8,128)(2,1)}, u32[]{:S(2)}) copy-start(bf16[512,1152]{0,1:T(8,128)(2,1)} %fusion.35) | copy-start | bytes 3538948
  997.8 18.4 %all-to-all-start.7 = ((bf16[2,512,576]{1,2,0:T(8,128)(2,1)}), bf16[2,512,576]{1,2,0:T(8,128)(2,1)S(1)}, u32[]{:S(2)}, u32[]{:S(2)}) async-start(bf16[2,512,576]{1,2,0:T(8,128)(2,1)} %bitcast.28), calls=%async_computation.7 | async-start | bytes 2359296 | tf_op jit(solution)/shard_map/all_to_all | solution.py:38
Sparse Core Ops, SparseCore 0:
  11.8 114.9 all-gather.11
  130.6 100.1 all-gather.13
  234.4 115.1 all-gather.21
  353.1 119.4 all-gather.19
  476.0 116.5 all-gather.15
  596.1 116.5 all-gather.17
  716.3 127.0 all-gather.23
  847.0 127.0 all-gather.25
where the time goes:
time: 1030 us; the launch traced here: 1020 us
  waiting for transfers between devices  842 us (82%)
  local copies, waits for them, and re-layouts  71.3 us (7%)
  matrix products  46.9 us (5%)
  starting transfers between devices  30.7 us (3%)
  other arithmetic  18.8 us (2%)
  between operations  14.7 us (1%)
    all_gather x2, waiting for transfers between devices, encoder(): lax.all_gather(down_weight, 'dp', axis=1, tiled=True)  242 us
    all_gather x2, waiting for transfers between devices, encoder(): lax.all_gather(qkv_weight, 'dp', axis=0, tiled=True)  209 us
    all_gather x2, waiting for transfers between devices, encoder(): lax.all_gather(out_weight, 'dp', axis=1, tiled=True)  169 us
    all_gather x2, waiting for transfers between devices, encoder(): lax.all_gather(up_weight, 'dp', axis=0, tiled=True)  167 us
    all_to_all x4, waiting for transfers between devices, sum_at_owner(): lax.all_to_all(pieces, axis, split_axis=0, concat_axis=0, tiled=True)  38.1 us
    dot_general x2, matrix products, encoder(): jnp.dot(hidden, lax.all_gather(down_weight, 'dp', axis=1, tiled=True), pr...  30.1 us
    unnamed x29, local copies, waits for them, and re-layouts  28.5 us
  transfers between devices with their start and end apart: 16, of which 12 were waited for; matrix products, arithmetic and copies ran while one was open for 13% of the time, Pallas kernels for 0%

commit v1 on v0

--- a/solution.py
+++ b/solution.py
@@ -59,7 +59,12 @@
         count = piece.shape[0]
         return jnp.dot(source, piece.reshape(count, -1), preferred_element_type=jnp.float32)
 
-    qkv = fold_rows(normed, lax.all_gather(qkv_weight, "dp", axis=0, tiled=True))
+    qkv = fold_rows(
+        normed,
+        jnp.concatenate(
+            lax.all_to_all(jnp.stack([qkv_weight] * lax.axis_size("dp")), "dp", 0, 0), axis=0
+        ),
+    )
     qkv = qkv.astype(jnp.bfloat16).reshape(rows // PATCHES, PATCHES, 3, local_heads, head_size)
     query = qkv[:, :, 0]
     keys = qkv[:, :, 1]

time: 1030 us -> 830 us (0.81)
  waiting for transfers between devices: 842 us -> 583 us
  blocking collectives: 0 us -> 41 us
  starting transfers between devices: 30.7 us -> 52.3 us
    all_gather x2 -> x0, waiting for transfers between devices: 209 us -> none  [encoder(): lax.all_gather(qkv_weight, 'dp', axis=0, tiled=True)]
    all_to_all x0 -> x2, waiting for transfers between devices: none -> 159 us  [encoder(): lax.all_to_all(jnp.stack([qkv_weight] * lax.axis_size('dp')), 'dp', 0, 0)]
    all_gather x2, waiting for transfers between devices: 169 us -> 50.6 us  [encoder(): lax.all_gather(out_weight, 'dp', axis=1, tiled=True)]
    all_gather x2, waiting for transfers between devices: 167 us -> 107 us  [encoder(): lax.all_gather(up_weight, 'dp', axis=0, tiled=True)]
    all_to_all x0 -> x3, blocking collectives: none -> 41 us  [the longest x2 26.3 us: from_everyone(): lax.all_to_all(jnp.broadcast_to(shard[None], (size, *shard.shape)), axis,...]
    all_to_all x0 -> x2, starting transfers between devices: none -> 33.5 us  [encoder(): lax.all_to_all(jnp.stack([qkv_weight] * lax.axis_size('dp')), 'dp', 0, 0)]
    another operation x0 -> x3, local copies, waits for them, and re-layouts: none -> 18.2 us  [the longest x1 12.4 us: fold_rows(): piece.reshape(count, -1)]
    all_gather x2 -> x0, local copies, waits for them, and re-layouts: 16 us -> none  [encoder(): lax.all_gather(qkv_weight, 'dp', axis=0, tiled=True)]
  transfers between devices with their start and end apart: 16 -> 13, of which waited for: 12 -> 9; matrix products, arithmetic and copies ran while one was open for 13% -> 16% of each run, Pallas kernels for 0% -> 0%
where the time goes in v1:
time: 830 us; the launch traced here: 820 us
  waiting for transfers between devices  583 us (70%)
  local copies, waits for them, and re-layouts  67.3 us (8%)
  starting transfers between devices  52.3 us (6%)
  matrix products  45.6 us (5%)
  blocking collectives  41 us (5%)
  other arithmetic  16.4 us (2%)
  between operations  14.7 us (2%)
    all_gather x2, waiting for transfers between devices, encoder(): lax.all_gather(down_weight, 'dp', axis=1, tiled=True)  227 us
    all_to_all x2, waiting for transfers between devices, encoder(): lax.all_to_all(jnp.stack([qkv_weight] * lax.axis_size('dp')), 'dp', 0, 0)  159 us
    all_gather x2, waiting for transfers between devices, encoder(): lax.all_gather(up_weight, 'dp', axis=0, tiled=True)  107 us
    all_gather x2, waiting for transfers between devices, encoder(): lax.all_gather(out_weight, 'dp', axis=1, tiled=True)  50.6 us
    all_to_all x2, starting transfers between devices, encoder(): lax.all_to_all(jnp.stack([qkv_weight] * lax.axis_size('dp')), 'dp', 0, 0)  33.5 us
    unnamed x33, local copies, waits for them, and re-layouts  29.2 us
    dot_general x2, matrix products, encoder(): jnp.dot(hidden, lax.all_gather(down_weight, 'dp', axis=1, tiled=True), pr...  29.1 us
    all_to_all x2, blocking collectives, from_everyone(): lax.all_to_all(jnp.broadcast_to(shard[None], (size, *shard.shape)), axis,...  26.3 us
  transfers between devices with their start and end apart: 13, of which 9 were waited for; matrix products, arithmetic and copies ran while one was open for 16% of the time, Pallas kernels for 0%

profile of v1, /device:TPU:1, one launch (start us, length us, event | category | flops | bytes accessed | tf_op | source)
XLA Modules:
  0.0 820.3 jit_solution(4557272339010694307)
XLA Ops:
  11.3 14.2 %all_to_all.50 = bf16[2,512,512]{1,2,0:T(8,128)(2,1)S(1)} all-to-all(bf16[2,512,512]{1,2,0:T(8,128)(2,1)S(1)} %broadcast_in_dim.8), channel_id=1, replica_groups=mesh['dp'=128,'mp'=2] {'mp'}, dimensions={0} | all-to-all | bytes 2097152 | tf_op jit(solution)/shard_map/all_to_all | solution.py:14
  27.4 18.9 %all-to-all-start.1 = ((bf16[128,8,3,512]{3,1,2,0:T(8,128)(2,1)}), bf16[128,8,3,512]{3,1,2,0:T(8,128)(2,1)}, u32[]{:S(2)}, u32[]{:S(2)}) async-start(bf16[128,8,3,512]{3,1,2,0:T(8,128)(2,1)} %stack.4), calls=%async_computation.1 | async-start | bytes 6291456 | tf_op jit(solution)/shard_map/all_to_all | solution.py:65
  47.8 75.3 %all-to-all-done.1 = bf16[128,8,3,512]{3,1,2,0:T(8,128)(2,1)} async-done(((bf16[128,8,3,512]{3,1,2,0:T(8,128)(2,1)}), bf16[128,8,3,512]{3,1,2,0:T(8,128)(2,1)}, u32[]{:S(2)}, u32[]{:S(2)}) %all-to-all-start.1) | async-done | bytes 3145760 | tf_op jit(solution)/shard_map/all_to_all | solution.py:65
  123.1 4.9 convolution_convert_fusion.2
  128.0 4.0 reshape.168
  139.8 3.2 fusion.103
  146.3 14.7 %all_to_all.51 = bf16[2,512,512]{2,1,0:T(8,128)(2,1)S(1)} all-to-all(bf16[2,512,512]{2,1,0:T(8,128)(2,1)S(1)} %bitcast.103), channel_id=1, replica_groups=mesh['dp'=128,'mp'=2] {'mp'}, dimensions={0} | all-to-all | bytes 2097152 | tf_op jit(solution)/shard_map/all_to_all | solution.py:38
  162.2 3.6 all-to-all-start.5
  166.4 12.1 %all-to-all-done.5 = bf16[2,512,576]{1,2,0:T(8,128)(2,1)S(1)} async-done(((bf16[2,512,576]{1,2,0:T(8,128)(2,1)}), bf16[2,512,576]{1,2,0:T(8,128)(2,1)S(1)}, u32[]{:S(2)}, u32[]{:S(2)}) %all-to-all-start.5) | async-done | bytes 1179680 | tf_op jit(solution)/shard_map/all_to_all | solution.py:14
  178.5 12.1 %all_to_all.52 = bf16[2,512,512]{1,2,0:T(8,128)(2,1)S(1)} all-to-all(bf16[2,512,512]{1,2,0:T(8,128)(2,1)S(1)} %broadcast_in_dim.9), channel_id=1, replica_groups=mesh['dp'=128,'mp'=2] {'mp'}, dimensions={0} | all-to-all | bytes 2097152 | tf_op jit(solution)/shard_map/all_to_all | solution.py:14
  190.7 4.0 stack.5
  194.7 14.6 %all-to-all-start.6 = ((bf16[128,9,3,576]{3,2,1,0:T(4,128)(2,1)}), bf16[128,9,3,576]{3,2,1,0:T(4,128)(2,1)}, u32[]{:S(2)}, u32[]{:S(2)}) async-start(bf16[128,9,3,576]{3,2,1,0:T(4,128)(2,1)} %stack.5), calls=%async_computation.6 | async-start | bytes 11796480 | tf_op jit(solution)/shard_map/all_to_all | solution.py:65
  211.9 50.6 %all-gather.16.cloned.1.call-done = bf16[128,9,576]{2,1,0:T(8,128)(2,1)} async-done(((bf16[1,9,576]{2,1,0:T(8,128)(2,1)}), bf16[128,9,576]{2,1,0:T(8,128)(2,1)}) %all-gather.16.cloned.1.call-update) | async-done | bytes 1327120 | tf_op jit(solution)/shard_map/all_gather | solution.py:80
  262.5 4.1 reshape.163
  266.8 83.5 %all-to-all-done.6 = bf16[128,9,3,576]{3,2,1,0:T(4,128)(2,1)} async-done(((bf16[128,9,3,576]{3,2,1,0:T(4,128)(2,1)}), bf16[128,9,3,576]{3,2,1,0:T(4,128)(2,1)}, u32[]{:S(2)}, u32[]{:S(2)}) %all-to-all-start.6) | async-done | bytes 3981344 | tf_op jit(solution)/shard_map/all_to_all | solution.py:65
  350.3 12.4 %reshape_reshape.7 = bf16[1152,1728]{1,0:T(8,128)(2,1)} reshape(bf16[128,9,3,576]{3,2,1,0:T(4,128)(2,1)} %all-to-all-done.6) | data formatting | bytes 7962624 | tf_op jit(solution)/shard_map/reshape;reshape | solution.py:60
  362.6 6.0 convolution_convert_fusion.1
  368.6 3.9 reshape.156
  374.5 3.2 fusion.104
  381.8 3.7 all-to-all-start.7
  387.2 10.7 %all-to-all-done.7 = bf16[2,512,576]{1,2,0:T(8,128)(2,1)S(1)} async-done(((bf16[2,512,576]{1,2,0:T(8,128)(2,1)}), bf16[2,512,576]{1,2,0:T(8,128)(2,1)S(1)}, u32[]{:S(2)}, u32[]{:S(2)}) %all-to-all-start.7) | async-done | bytes 1179680 | tf_op jit(solution)/shard_map/all_to_all | solution.py:38
  399.5 4.0 all-to-all-start.8
  403.6 105.2 %all-gather.14.cloned.1.call-done = bf16[2048,1024]{0,1:T(8,128)(2,1)} async-done(((bf16[2048,8]{0,1:T(8,128)(2,1)}), bf16[2048,1024]{0,1:T(8,128)(2,1)}) %all-gather.14.cloned.1.call-update) | async-done | bytes 4194320 | tf_op jit(solution)/shard_map/all_gather | solution.py:91
  508.8 16.9 %fusion.53 = bf16[512,1024]{1,0:T(8,128)(2,1)S(1)} fusion(bf16[2048,1024]{0,1:T(8,128)(2,1)} %all-gather.14.cloned.1.call-done, bf16[512,1024]{0,1:T(8,128)(2,1)} %fusion.46, bf16[1024,2048]{1,0:T(8,128)(2,1)} %all-gather.12.cloned.1.call-done), kind=kOutput, calls=%fused_computation.79 | convolution fusion | flops 4363649024 | bytes 10485760 | tf_op jit(solution)/shard_map/dot_general | solution.py:89
  526.8 3.6 all-to-all-start.4
  532.4 106.9 %all-gather.18.cloned.1.call-done = bf16[128,9,2152]{2,1,0:T(8,128)(2,1)} async-done(((bf16[1,9,2152]{2,1,0:T(8,128)(2,1)}), bf16[128,9,2152]{2,1,0:T(8,128)(2,1)}) %all-gather.18.cloned.1.call-update) | async-done | bytes 4958224 | tf_op jit(solution)/shard_map/all_gather | solution.py:87
  639.3 9.2 %reshape.165 = bf16[1152,2152]{1,0:T(8,128)(2,1)} reshape(bf16[128,9,2152]{2,1,0:T(8,128)(2,1)} %all-gather.18.cloned.1.call-done) | data formatting | bytes 9916416
  648.5 121.3 %all-gather.20.cloned.1.call-done = bf16[128,9,2152]{2,1,0:T(8,128)(2,1)} async-done(((bf16[1,9,2152]{2,1,0:T(8,128)(2,1)}), bf16[128,9,2152]{2,1,0:T(8,128)(2,1)}) %all-gather.20.cloned.1.call-update) | async-done | bytes 4958224 | tf_op jit(solution)/shard_map/all_gather | solution.py:91
  769.8 9.1 %reshape.167 = bf16[1152,2152]{1,0:T(8,128)(2,1)} reshape(bf16[128,9,2152]{2,1,0:T(8,128)(2,1)} %all-gather.20.cloned.1.call-done) | data formatting | bytes 9916416
  779.0 12.2 %convolution_convert_fusion.3 = bf16[512,1152]{1,0:T(8,128)(2,1)} fusion(bf16[1152,2152]{1,0:T(8,128)(2,1)} %reshape.167, bf16[512,1152]{0,1:T(8,128)(2,1)S(1)} %copy-done.5, bf16[1152,2152]{1,0:T(8,128)(2,1)} %reshape.165), kind=kOutput, calls=%fused_computation.41 | convolution fusion | flops 5087711232 | bytes 12275712 | tf_op jit(solution)/shard_map/dot_general | solution.py:89
  793.5 3.6 all-to-all-start.9
  798.3 13.7 %all-to-all-done.9 = bf16[2,512,576]{1,2,0:T(8,128)(2,1)S(1)} async-done(((bf16[2,512,576]{1,2,0:T(8,128)(2,1)}), bf16[2,512,576]{1,2,0:T(8,128)(2,1)S(1)}, u32[]{:S(2)}, u32[]{:S(2)}) %all-to-all-start.9) | async-done | bytes 1179680 | tf_op jit(solution)/shard_map/all_to_all | solution.py:38
  (96 shorter events, 40.2 us)
Async XLA Ops:
  7.2 18.4 %copy-start.7 = (bf16[8,3,512]{2,0,1:T(8,128)(2,1)S(1)}, bf16[8,3,512]{2,0,1:T(8,128)(2,1)}, u32[]{:S(2)}) copy-start(bf16[8,3,512]{2,0,1:T(8,128)(2,1)} %param.17) | copy-start | bytes 73732
  7.2 137.0 %all-gather.10.cloned.1.call-start = ((), (), s32[]{:S(2)}) async-start(), calls=%async_computation.10 | async-start | bytes 1056768 | tf_op jit(solution)/shard_map/all_gather | solution.py:80
  7.9 254.6 %all-gather.16.cloned.1.call-start = ((), (), s32[]{:S(2)}) async-start(), calls=%async_computation.13 | async-start | bytes 2641920 | tf_op jit(solution)/shard_map/all_gather | solution.py:80
  8.7 394.9 %all-gather.12.cloned.1.call-start = ((), (), s32[]{:S(2)}) async-start(), calls=%async_computation.11 | async-start | bytes 4227072 | tf_op jit(solution)/shard_map/all_gather | solution.py:87
  9.4 499.4 %all-gather.14.cloned.1.call-start = ((), (), s32[]{:S(2)}) async-start(), calls=%async_computation.12 | async-start | bytes 4227072 | tf_op jit(solution)/shard_map/all_gather | solution.py:91
  25.5 21.4 %copy-start.11 = (f32[1024]{0:T(1024)S(1)}, f32[1024]{0:T(1024)}, u32[]{:S(2)}) copy-start(f32[1024]{0:T(1024)} %param.16) | copy-start | bytes 12292
  27.4 95.7 %all-to-all-start.1 = ((bf16[128,8,3,512]{3,1,2,0:T(8,128)(2,1)}), bf16[128,8,3,512]{3,1,2,0:T(8,128)(2,1)}, u32[]{:S(2)}, u32[]{:S(2)}) async-start(bf16[128,8,3,512]{3,1,2,0:T(8,128)(2,1)} %stack.4), calls=%async_computation.1 | async-start | bytes 6291456 | tf_op jit(solution)/shard_map/all_to_all | solution.py:65
  46.3 593.0 %all-gather.18.cloned.1.call-start = ((), (), s32[]{:S(2)}) async-start(), calls=%async_computation.14 | async-start | bytes 8982528 | tf_op jit(solution)/shard_map/all_gather | solution.py:87
  144.1 17.0 %copy-start = (bf16[512,576]{0,1:T(8,128)(2,1)S(1)}, bf16[512,576]{0,1:T(8,128)(2,1)}, u32[]{:S(2)}) copy-start(bf16[512,576]{0,1:T(8,128)(2,1)} %param.15) | copy-start | bytes 1769476
  146.3 19.7 %copy-start.2 = (bf16[512,512]{1,0:T(8,128)(2,1)S(1)}, bf16[512,512]{1,0:T(8,128)(2,1)}, u32[]{:S(2)}) copy-start(bf16[512,512]{1,0:T(8,128)(2,1)} %param.14) | copy-start | bytes 1572868
  162.2 16.3 %all-to-all-start.5 = ((bf16[2,512,576]{1,2,0:T(8,128)(2,1)}), bf16[2,512,576]{1,2,0:T(8,128)(2,1)S(1)}, u32[]{:S(2)}, u32[]{:S(2)}) async-start(bf16[2,512,576]{1,2,0:T(8,128)(2,1)} %broadcast_in_dim.10), calls=%async_computation.5 | async-start | bytes 2359296 | tf_op jit(solution)/shard_map/all_to_all | solution.py:14
  165.8 24.8 %copy-start.6 = (bf16[9,3,576]{2,1,0:T(4,128)(2,1)S(1)}, bf16[9,3,576]{2,1,0:T(4,128)(2,1)}, u32[]{:S(2)}) copy-start(bf16[9,3,576]{2,1,0:T(4,128)(2,1)} %param.23) | copy-start | bytes 93316
  194.7 15.2 %copy-start.9 = (f32[1152]{0:T(1024)S(1)}, f32[1152]{0:T(1024)}, u32[]{:S(2)}) copy-start(f32[1152]{0:T(1024)} %param.22) | copy-start | bytes 13828
  194.7 155.6 %all-to-all-start.6 = ((bf16[128,9,3,576]{3,2,1,0:T(4,128)(2,1)}), bf16[128,9,3,576]{3,2,1,0:T(4,128)(2,1)}, u32[]{:S(2)}, u32[]{:S(2)}) async-start(bf16[128,9,3,576]{3,2,1,0:T(4,128)(2,1)} %stack.5), calls=%async_computation.6 | async-start | bytes 11796480 | tf_op jit(solution)/shard_map/all_to_all | solution.py:65
  209.3 560.5 %all-gather.20.cloned.1.call-start = ((), (), s32[]{:S(2)}) async-start(), calls=%async_computation.15 | async-start | bytes 8982528 | tf_op jit(solution)/shard_map/all_gather | solution.py:91
  266.8 95.8 %copy-start.4 = (bf16[2,512,576]{1,2,0:T(8,128)(2,1)S(1)}, bf16[2,512,576]{1,2,0:T(8,128)(2,1)}, u32[]{:S(2)}) copy-start(bf16[2,512,576]{1,2,0:T(8,128)(2,1)} %fusion.32) | copy-start | bytes 3538948
  377.8 1.4 copy-start.3
  379.1 6.8 copy-start.10
  381.8 16.3 %copy-start.1 = (bf16[512,576]{0,1:T(8,128)(2,1)S(1)}, bf16[512,576]{0,1:T(8,128)(2,1)}, u32[]{:S(2)}) copy-start(bf16[512,576]{0,1:T(8,128)(2,1)} %param.15) | copy-start | bytes 1769476
  381.8 16.1 %all-to-all-start.7 = ((bf16[2,512,576]{1,2,0:T(8,128)(2,1)}), bf16[2,512,576]{1,2,0:T(8,128)(2,1)S(1)}, u32[]{:S(2)}, u32[]{:S(2)}) async-start(bf16[2,512,576]{1,2,0:T(8,128)(2,1)} %bitcast.20), calls=%async_computation.7 | async-start | bytes 2359296 | tf_op jit(solution)/shard_map/all_to_all | solution.py:38
  399.5 127.3 %all-to-all-start.8 = ((bf16[2,512,576]{1,2,0:T(8,128)(2,1)}), bf16[2,512,576]{1,2,0:T(8,128)(2,1)S(1)}, u32[]{:S(2)}, u32[]{:S(2)}) async-start(bf16[2,512,576]{1,2,0:T(8,128)(2,1)} %broadcast_in_dim.11), calls=%async_computation.8 | async-start | bytes 2359296 | tf_op jit(solution)/shard_map/all_to_all | solution.py:14
  525.7 5.3 copy-start.8
  526.8 266.8 %all-to-all-start.4 = ((bf16[2,512,512]{2,1,0:T(8,128)(2,1)}), bf16[2,512,512]{2,1,0:T(8,128)(2,1)S(1)}, u32[]{:S(2)}, u32[]{:S(2)}) async-start(bf16[2,512,512]{2,1,0:T(8,128)(2,1)} %bitcast.102), calls=%async_computation.4 | async-start | bytes 2097152 | tf_op jit(solution)/shard_map/all_to_all | solution.py:38
  648.5 130.5 %copy-start.5 = (bf16[512,1152]{0,1:T(8,128)(2,1)S(1)}, bf16[512,1152]{0,1:T(8,128)(2,1)}, u32[]{:S(2)}) copy-start(bf16[512,1152]{0,1:T(8,128)(2,1)} %fusion.35) | copy-start | bytes 3538948
  793.5 18.4 %all-to-all-start.9 = ((bf16[2,512,576]{1,2,0:T(8,128)(2,1)}), bf16[2,512,576]{1,2,0:T(8,128)(2,1)S(1)}, u32[]{:S(2)}, u32[]{:S(2)}) async-start(bf16[2,512,576]{1,2,0:T(8,128)(2,1)} %bitcast.27), calls=%async_computation.9 | async-start | bytes 2359296 | tf_op jit(solution)/shard_map/all_to_all | solution.py:38
Sparse Core Ops, SparseCore 0:
  11.7 116.2 all-gather.9
  131.6 130.8 all-gather.15
  266.1 122.5 all-gather.11
  392.2 116.5 all-gather.13
  512.2 127.0 all-gather.17
  642.8 127.0 all-gather.19
